TPU v7x, 32 devices: a whole 2x2x4 slice. The times are simulated.
32 devices in a mesh: rep: 16 (over z, x, core), tp: 2 (over y).
Axes of the slice: x: 2, y: 2, z: 4, core: 2. Of those that a mesh axis runs over, the one named last changes fastest.
Arguments:
- tokens: bfloat16 [16, 256, 3072], P('rep', 'tp'), may hold values from -100 to 100
- norm_gain: float32 [16, 3072], P('rep'), may hold values from 0.5 to 1.5
- w_query: bfloat16 [16, 3072, 2048], P('rep', None, 'tp'), may hold values from -1 to 1
- key_weight: bfloat16 [16, 3072, 1024], P('rep', None, 'tp'), may hold values from -1 to 1
- value_weight: bfloat16 [16, 3072, 1024], P('rep', None, 'tp'), may hold values from -0.109375 to 0.109375
- attention_gradient: bfloat16 [16, 256, 2048], P('rep', None, 'tp'), may hold values from -6 to 6
- global_fragment: float32 [128, 3072], P('tp'), may hold values from -6 to 6
- momentum: float32 [128, 3072], P('tp'), may hold values from -3 to 3
- local_fragment: bfloat16 [16, 128, 3072], P('rep', 'tp'), may hold values from -6 to 6
Outputs:
- grad_query_w: bfloat16 [16, 3072, 2048], P('rep', None, 'tp')
- grad_key_w: bfloat16 [16, 3072, 1024], P('rep', None, 'tp')
- grad_value_w: bfloat16 [16, 3072, 1024], P('rep', None, 'tp')
- grad_gain: float32 [16, 3072], P('rep')
- grad_tokens: bfloat16 [16, 256, 3072], P('rep', 'tp')
- new_global: float32 [128, 3072], P('tp')
- new_momentum: float32 [128, 3072], P('tp')
All inputs are finite; a program needn't handle non-finite values.
Results may differ from a plain program's by a relative error of at most 0.019.
The roundings to bfloat16 on the way count: a program that leaves them out, or rounds other values in their place, can miss the bound.
Values may be sent and summed in bfloat16 or wider, within the bound.
A program may use at most 128 MiB of HBM per device.

v0:
```python
import jax
import jax.numpy as jnp
from jax import lax
from jax.sharding import PartitionSpec as P

HEAD_SIZE = 128
epsilon = 1e-05
rope_base = 500000.0
outer_rate = 0.7
outer_momentum = 0.9


def rope_tables(sequence_length, width):
    middle = width // 2
    frequency = rope_base ** (-2.0 * jnp.arange(middle, dtype=jnp.float32) / width)
    angles = jnp.arange(sequence_length, dtype=jnp.float32)[:, None] * frequency[None, :]
    angles = jnp.concatenate([angles, angles], axis=1)
    return (jnp.cos(angles)[:, None, :], jnp.sin(angles)[:, None, :])


def rotate(vectors, cosine_table, sine_table):
    middle = vectors.shape[-1] // 2
    turned = jnp.concatenate([-vectors[..., middle:], vectors[..., :middle]], axis=-1)
    return vectors * cosine_table + turned * sine_table


def reverse_rotation(gradient, cosine_table, sine_table):
    middle = gradient.shape[-1] // 2
    shifted = gradient * sine_table
    turned = jnp.concatenate([shifted[..., middle:], -shifted[..., :middle]], axis=-1)
    return gradient * cosine_table + turned


def attention_reverse(query_rows, rotated_keys, values_bfloat, grad_out, block_of_rows):
    sequence_length = query_rows.shape[0]
    score_scale = query_rows.shape[-1] ** (-0.5)

    def one_block(running, block_index):
        acc_key, acc_value = running
        offset = block_index * block_of_rows
        query_block = lax.dynamic_slice_in_dim(query_rows, offset, block_of_rows, 0)
        grad_block = lax.dynamic_slice_in_dim(grad_out, offset, block_of_rows, 0)
        scores = (
            jnp.einsum(
                "qgrd,kgd->grqk", query_block, rotated_keys, preferred_element_type=jnp.float32
            )
            * score_scale
        )
        row_pos = offset + jnp.arange(block_of_rows)
        col_pos = jnp.arange(sequence_length)
        allowed = col_pos[None, :] <= row_pos[:, None]
        scores = jnp.where(allowed, scores, -jnp.inf)
        highest = jnp.max(scores, axis=-1, keepdims=True)
        powers = jnp.exp(scores - highest)
        probability = powers / jnp.sum(powers, axis=-1, keepdims=True)
        prob_low = probability.astype(jnp.bfloat16)
        acc_value = acc_value + jnp.einsum(
            "grqk,qgrd->kgd", prob_low, grad_block, preferred_element_type=jnp.float32
        )
        grad_prob = jnp.einsum(
            "qgrd,kgd->grqk", grad_block, values_bfloat, preferred_element_type=jnp.float32
        )
        grad_score = (
            probability
            * (grad_prob - jnp.sum(grad_prob * probability, axis=-1, keepdims=True))
            * score_scale
        )
        score_low = grad_score.astype(jnp.bfloat16)
        grad_query = jnp.einsum(
            "grqk,kgd->qgrd", score_low, rotated_keys, preferred_element_type=jnp.float32
        )
        acc_key = acc_key + jnp.einsum(
            "grqk,qgrd->kgd", score_low, query_block, preferred_element_type=jnp.float32
        )
        return ((acc_key, acc_value), grad_query)

    initial = jnp.zeros(rotated_keys.shape, jnp.float32)
    (acc_key, acc_value), grad_blocks = lax.scan(
        one_block, (initial, initial), jnp.arange(sequence_length // block_of_rows)
    )
    return (grad_blocks.reshape(query_rows.shape), acc_key, acc_value)


def body(
    tokens,
    norm_gain,
    w_query,
    key_weight,
    value_weight,
    attention_gradient,
    global_fragment,
    momentum,
    local_fragment,
):
    local_rows = tokens[0]
    norm_gains = norm_gain[0]
    weight_q = w_query[0]
    weight_k = key_weight[0]
    weight_v = value_weight[0]
    widened_rows = local_rows.astype(jnp.float32)
    inverse_norm = lax.rsqrt(
        jnp.mean(widened_rows * widened_rows, axis=-1, keepdims=True) + epsilon
    )
    normalized_input = widened_rows * inverse_norm
    normalized_local = (normalized_input * norm_gains[None, :]).astype(jnp.bfloat16)
    normalized = lax.all_gather(normalized_local, "tp", axis=0, tiled=True)
    sequence_length = normalized.shape[0]
    heads_q = weight_q.shape[1] // HEAD_SIZE
    heads_kv = weight_k.shape[1] // HEAD_SIZE
    cosine_table, sine_table = rope_tables(sequence_length, HEAD_SIZE)
    query_rows = jnp.dot(normalized, weight_q, preferred_element_type=jnp.float32).reshape(
        sequence_length, heads_q, HEAD_SIZE
    )
    query_rows = rotate(query_rows, cosine_table, sine_table).astype(jnp.bfloat16)
    rotated_keys = jnp.dot(normalized, weight_k, preferred_element_type=jnp.float32).reshape(
        sequence_length, heads_kv, HEAD_SIZE
    )
    rotated_keys = rotate(rotated_keys, cosine_table, sine_table).astype(jnp.bfloat16)
    values_bfloat = (
        jnp.dot(normalized, weight_v, preferred_element_type=jnp.float32)
        .astype(jnp.bfloat16)
        .reshape(sequence_length, heads_kv, HEAD_SIZE)
    )
    replica_group = heads_q // heads_kv
    block_of_rows = min(512, sequence_length)
    query_input_gradient, key_input_gradient, value_input_gradient = attention_reverse(
        query_rows.reshape(sequence_length, heads_kv, replica_group, HEAD_SIZE),
        rotated_keys,
        values_bfloat,
        attention_gradient[0].reshape(sequence_length, heads_kv, replica_group, HEAD_SIZE),
        block_of_rows,
    )
    dquery = (
        reverse_rotation(
            query_input_gradient.reshape(sequence_length, heads_q, HEAD_SIZE),
            cosine_table,
            sine_table,
        )
        .astype(jnp.bfloat16)
        .reshape(sequence_length, heads_q * HEAD_SIZE)
    )
    key_gradient = (
        reverse_rotation(key_input_gradient, cosine_table, sine_table)
        .astype(jnp.bfloat16)
        .reshape(sequence_length, heads_kv * HEAD_SIZE)
    )
    value_gradient = value_input_gradient.astype(jnp.bfloat16).reshape(
        sequence_length, heads_kv * HEAD_SIZE
    )
    contract = (((0,), (0,)), ((), ()))
    grad_wq = lax.dot_general(
        normalized, dquery, contract, preferred_element_type=jnp.float32
    ).astype(jnp.bfloat16)
    grad_wk = lax.dot_general(
        normalized, key_gradient, contract, preferred_element_type=jnp.float32
    ).astype(jnp.bfloat16)
    grad_wv = lax.dot_general(
        normalized, value_gradient, contract, preferred_element_type=jnp.float32
    ).astype(jnp.bfloat16)
    back = (((1,), (1,)), ((), ()))
    partial_value = lax.dot_general(dquery, weight_q, back, preferred_element_type=jnp.float32)
    partial_value = partial_value + lax.dot_general(
        key_gradient, weight_k, back, preferred_element_type=jnp.float32
    )
    summed_rows = lax.psum_scatter(
        (
            partial_value
            + lax.dot_general(value_gradient, weight_v, back, preferred_element_type=jnp.float32)
        ).astype(jnp.bfloat16),
        "tp",
        scatter_dimension=0,
        tiled=True,
    ).astype(jnp.float32)
    gains_gradient = lax.psum(jnp.sum(summed_rows * normalized_input, axis=0), "tp")
    scaled_rows = summed_rows * norm_gains[None, :]
    gradient_rows = (
        inverse_norm
        * (
            scaled_rows
            - normalized_input * jnp.mean(scaled_rows * normalized_input, axis=-1, keepdims=True)
        )
    ).astype(jnp.bfloat16)
    delta = global_fragment - local_fragment[0].astype(jnp.float32)
    replicas = lax.axis_size("rep")
    mean_delta = lax.psum(delta, "rep") / replicas
    new_momentum = outer_momentum * momentum + mean_delta
    new_global = global_fragment - outer_rate * (mean_delta + outer_momentum * new_momentum)
    return (
        grad_wq[None],
        grad_wk[None],
        grad_wv[None],
        gains_gradient[None],
        gradient_rows[None],
        new_global,
        new_momentum,
    )


def solution(mesh):
    placed = (
        P("rep", "tp", None),
        P("rep", None),
        P("rep", None, "tp"),
        P("rep", None, "tp"),
        P("rep", None, "tp"),
        P("rep", None, "tp"),
        P("tp", None),
        P("tp", None),
        P("rep", "tp", None),
    )
    return jax.shard_map(
        body,
        mesh=mesh,
        in_specs=placed,
        out_specs=(
            P("rep", None, "tp"),
            P("rep", None, "tp"),
            P("rep", None, "tp"),
            P("rep", None),
            P("rep", "tp", None),
            P("tp", None),
            P("tp", None),
        ),
        check_vma=False,
    )
```

profile of v0, /device:TPU:0, one launch (start us, length us, event | category | flops | bytes accessed | tf_op | source)
XLA Modules:
  0.0 146.9 jit_solution(9005998716346742518)
XLA Ops:
  9.6 2.3 %fusion.22 = bf16[128,3072]{1,0:T(8,128)(2,1)} fusion(bf16[1,128,3072]{2,1,0:T(8,128)(2,1)} %param.9, f32[3072]{0:T(1024)} %bitcast.153, f32[128]{0:T(128)S(1)} %add_rsqrt_fusion), kind=kLoop, calls=%fused_computation.34 | loop fusion | flops 1572864 | bytes 1585664 | tf_op jit(solution)/shard_map/convert_element_type | solution.py:105
  12.0 2.1 %convert_subtract_fusion = f32[64,3072]{1,0:T(8,128)} fusion(f32[64,3072]{1,0:T(8,128)} %param.15, bf16[1,64,3072]{2,1,0:T(8,128)(2,1)S(1)} %copy-done.19), kind=kLoop, calls=%fused_computation.65 | loop fusion | flops 393216 | bytes 1966080 | tf_op jit(solution)/shard_map/sub | solution.py:183
  14.2 8.7 %copy.38 = bf16[1024,3072]{1,0:T(8,128)(2,1)} copy(bf16[1024,3072]{0,1:T(8,128)(2,1)} %bitcast.138) | data formatting | bytes 12582912 | tf_op jit(solution)/shard_map/dot_general | solution.py:111
  23.4 4.7 %copy.35 = bf16[512,3072]{1,0:T(8,128)(2,1)} copy(bf16[512,3072]{0,1:T(8,128)(2,1)} %bitcast.137) | data formatting | bytes 6291456 | tf_op jit(solution)/shard_map/dot_general | solution.py:115
  28.1 2.0 %copy.41 = bf16[1,256,1024]{1,2,0:T(8,128)(2,1)} copy(bf16[1,256,1024]{2,1,0:T(8,128)(2,1)} %param.14) | data formatting | bytes 1048576 | tf_op jit(solution)/shard_map/reshape;squeeze | solution.py:130
  30.2 11.8 %all-gather.2.cloned.1.call-done = bf16[256,3072]{1,0:T(8,128)(2,1)} async-done(((bf16[128,3072]{1,0:T(8,128)(2,1)}), bf16[256,3072]{1,0:T(8,128)(2,1)}) %all-gather.2.cloned.1.call-update) | async-done | bytes 1572880 | tf_op jit(solution)/shard_map/all_gather | solution.py:106
  42.0 5.3 %fusion.26 = f32[256,8,128]{0,2,1:T(8,128)S(1)} fusion(bf16[8,128,3072]{2,1,0:T(8,128)(2,1)} %bitcast.141, bf16[256,3072]{1,0:T(8,128)(2,1)} %all-gather.2.cloned.1.call-done), kind=kOutput, calls=%fused_computation.38 | convolution fusion | flops 1610612736 | bytes 8912896 | tf_op jit(solution)/shard_map/dot_general | solution.py:111
  51.5 1.7 %fusion.30 = bf16[256,512]{1,0:T(8,128)(2,1)} fusion(bf16[256,3072]{1,0:T(8,128)(2,1)S(1)} %copy-done.1, bf16[1,3072,512]{2,1,0:T(8,128)(2,1)S(1)} %copy-done), kind=kOutput, calls=%fused_computation.44 | convolution fusion | flops 805437440 | bytes 4980736 | tf_op jit(solution)/shard_map/dot_general | solution.py:120
  55.0 2.7 %fusion.35 = bf16[256,8,128]{0,2,1:T(8,128)(2,1)} fusion(f32[256,8,64]{0,2,1:T(8,128)} %get-tuple-element.40, f32[256,8,64]{0,2,1:T(8,128)} %get-tuple-element.39, f32[256,8,128]{0,2,1:T(8,128)} %copy-done.7, f32[256,128]{0,1:T(8,128)S(1)} %get-tuple-element.46, f32[256,128]{0,1:T(8,128)S(1)} %get-tuple-element.45), kind=kLoop, calls=%fused_computation.48 | loop fusion | flops 1310720 | bytes 2883584 | tf_op jit(solution)/shard_map/convert_element_type | solution.py:114
  58.5 1.7 %fusion.51 = f32[4,256,256,2]{2,1,3,0:T(8,128)} fusion(bf16[256,4,2,128]{0,3,2,1:T(8,128)(2,1)S(1)} %bitcast.146, bf16[256,4,128,1]{2,1,0,3:T(4,128)(2,1)S(1)} %bitcast.149), kind=kOutput, calls=%fused_computation.78 | convolution fusion | flops 134217728 | bytes 2883584 | tf_op jit(solution)/shard_map/while/body/eval_jaxpr/qgrd,kgd->grqk/dot_general | solution.py:60
  60.2 3.3 %fusion.65 = (f32[4,2,256]{2,1,0:T(2,128)S(1)}, f32[4,2,256,256]{2,3,1,0:T(8,128)}) fusion(pred[256,256]{0,1:T(8,128)(4,1)S(1)} %iota_compare_fusion, bf16[256,4,128,1]{0,2,3,1:T(8,128)(2,1)} %fusion.50, bf16[256,4,2,128]{0,3,2,1:T(8,128)(2,1)} %bitcast.150), kind=kOutput, calls=%fused_computation.98 | convolution fusion | flops 136315136 | bytes 2957312 | tf_op jit(solution)/shard_map/while/body/eval_jaxpr/sub | solution.py:54
  63.5 5.4 %broadcast_multiply_fusion = (f32[256,4,128]{0,2,1:T(8,128)}, f32[256,4,128]{0,2,1:T(8,128)}) fusion(f32[256,128]{0,1:T(8,128)S(1)} %get-tuple-element.46, bf16[256,4,2,128]{0,3,2,1:T(8,128)(2,1)} %bitcast.151, f32[4,256,256,2]{2,1,3,0:T(8,128)} %fusion.51, f32[4,2,256,256]{2,3,1,0:T(8,128)} %get-tuple-element.48, f32[4,2,256]{2,1,0:T(2,128)S(1)} %get-tuple-element.47), kind=kOutput, calls=%fused_computation.81 | convolution fusion | flops 138021120 | bytes 5906432 | tf_op jit(solution)/shard_map/while/body/eval_jaxpr/grqk,qgrd->kgd/dot_general | solution.py:72
  68.8 5.3 %fusion.44 = f32[4,128,2,256]{3,1,2,0:T(8,128)} fusion(bf16[256,4,128,1]{0,2,3,1:T(8,128)(2,1)} %fusion.50, f32[4,256,256,2]{2,1,3,0:T(8,128)} %fusion.51, f32[4,2,256,256]{2,3,1,0:T(8,128)} %get-tuple-element.48, f32[4,2,256]{2,1,0:T(2,128)S(1)} %get-tuple-element.47), kind=kOutput, calls=%fused_computation.62 | convolution fusion | flops 137890048 | bytes 5513216 | tf_op jit(solution)/shard_map/while/body/eval_jaxpr/grqk,kgd->qgrd/dot_general | solution.py:69
  74.2 2.3 %fusion.33 = bf16[4,256,128]{1,2,0:T(8,128)(2,1)S(1)} fusion(bf16[256,4,2,128]{0,3,2,1:T(8,128)(2,1)} %bitcast.145, f32[4,2,256,256]{2,3,1,0:T(8,128)} %get-tuple-element.48, f32[4,2,256]{2,1,0:T(2,128)S(1)} %get-tuple-element.47), kind=kOutput, calls=%fused_computation.45 | convolution fusion | flops 135397376 | bytes 2891776 | tf_op jit(solution)/shard_map/while/body/eval_jaxpr/grqk,qgrd->kgd/dot_general | solution.py:57
  79.0 1.8 %fusion.2 = f32[256,3072]{1,0:T(8,128)S(1)} fusion(bf16[256,1024]{0,1:T(8,128)(2,1)S(1)} %bitcast.152, bf16[1,3072,1024]{2,1,0:T(8,128)(2,1)S(1)} %bitcast.140), kind=kOutput, calls=%fused_computation.2 | convolution fusion | flops 1610612736 | bytes 9961472 | tf_op jit(solution)/shard_map/dot_general | solution.py:161
  82.1 2.2 %fusion.6 = bf16[256,3072]{1,0:T(8,128)(2,1)} fusion(f32[256,3072]{1,0:T(8,128)S(1)} %convolution_add_fusion.1, bf16[256,512]{0,1:T(8,128)(2,1)S(1)} %bitcast.147, bf16[1,3072,512]{2,1,0:T(8,128)(2,1)S(1)} %copy-done), kind=kOutput, calls=%fused_computation.11 | convolution fusion | flops 806879232 | bytes 8126464 | tf_op jit(solution)/shard_map/dot_general | solution.py:168
  84.3 27.0 %all-reduce.2.cloned.1.call-done = f32[64,3072]{1,0:T(8,128)} async-done(((f32[64,3072]{1,0:T(8,128)}), f32[64,3072]{1,0:T(8,128)}) %all-reduce.2.cloned.1.call-update) | async-done | bytes 786448 | tf_op jit(solution)/shard_map/psum | solution.py:185
  111.3 3.1 %multiply_subtract_fusion = (f32[64,3072]{1,0:T(8,128)}, f32[64,3072]{1,0:T(8,128)}) fusion(f32[64,3072]{1,0:T(8,128)} %param.15, f32[64,3072]{1,0:T(8,128)} %all-reduce.2.cloned.1.call-done, f32[64,3072]{1,0:T(8,128)} %param.16), kind=kLoop, calls=%fused_computation.66 | loop fusion | flops 1376256 | bytes 3932160 | tf_op jit(solution)/shard_map/sub | solution.py:187
  115.9 2.9 %fusion.5 = bf16[1,3072,512]{2,1,0:T(8,128)(2,1)} fusion(bf16[256,3072]{1,0:T(8,128)(2,1)S(1)} %copy-done.2, bf16[256,512]{0,1:T(8,128)(2,1)S(1)} %bitcast.148), kind=kOutput, calls=%fused_computation.8 | convolution fusion | flops 806879232 | bytes 4980736 | tf_op jit(solution)/shard_map/dot_general | solution.py:157
  118.8 2.7 %fusion.4 = bf16[1,3072,512]{2,1,0:T(8,128)(2,1)} fusion(bf16[256,3072]{1,0:T(8,128)(2,1)S(1)} %copy-done.2, bf16[256,512]{0,1:T(8,128)(2,1)S(1)} %bitcast.144), kind=kOutput, calls=%fused_computation.7 | convolution fusion | flops 806879232 | bytes 4980736 | tf_op jit(solution)/shard_map/dot_general | solution.py:154
  121.5 4.6 %convert_bitcast_fusion = bf16[1,3072,1024]{2,1,0:T(8,128)(2,1)} fusion(bf16[256,3072]{1,0:T(8,128)(2,1)S(1)} %copy-done.2, bf16[256,1024]{0,1:T(8,128)(2,1)S(1)} %fusion.37), kind=kOutput, calls=%fused_computation.4 | convolution fusion | flops 1613758464 | bytes 8388608 | tf_op jit(solution)/shard_map/dot_general | solution.py:151
  126.1 1.9 %fusion.24 = (f32[128]{0:T(128)S(1)}, f32[3072]{0:T(1024)S(1)}) fusion(bf16[128,3072]{1,0:T(8,128)(2,1)} %reduce-scatter.2.cloned.1.call-done, bf16[1,128,3072]{2,1,0:T(8,128)(2,1)} %param.9, f32[3072]{0:T(1024)S(1)} %bitcast.154, f32[128]{0:T(128)S(1)} %add_rsqrt_fusion), kind=kLoop, calls=%fused_computation.36 | loop fusion | flops 3142528 | bytes 1598464 | tf_op jit(solution)/shard_map/reduce_sum | solution.py:180
  128.0 8.8 %psum.14 = f32[1,3072]{1,0:T(1,128)} all-reduce(f32[1,3072]{1,0:T(1,128)S(1)} %bitcast.156), channel_id=1, replica_groups=mesh['rep'=16,'tp'=2] {'tp'}, use_global_device_ids=true, to_apply=%region_6.7 | all-reduce | flops 3072 | bytes 24576 | tf_op jit(solution)/shard_map/psum | solution.py:174
  136.8 2.7 %fusion.46 = bf16[1,128,3072]{2,1,0:T(8,128)(2,1)} fusion(bf16[128,3072]{1,0:T(8,128)(2,1)} %reduce-scatter.2.cloned.1.call-done, bf16[1,128,3072]{2,1,0:T(8,128)(2,1)} %param.9, f32[128]{0:T(128)S(1)} %broadcast_multiply_fusion.1, f32[3072]{0:T(1024)S(1)} %bitcast.155, f32[128]{0:T(128)S(1)} %add_rsqrt_fusion), kind=kLoop, calls=%fused_computation.64 | loop fusion | flops 3145728 | bytes 2372608 | tf_op jit(solution)/shard_map/broadcast_in_dim | solution.py:193
  (73 shorter events, 14.2 us)
Async XLA Ops:
  8.0 43.5 %copy-start = (bf16[1,3072,512]{2,1,0:T(8,128)(2,1)S(1)}, bf16[1,3072,512]{2,1,0:T(8,128)(2,1)}, u32[]{:S(2)}) copy-start(bf16[1,3072,512]{2,1,0:T(8,128)(2,1)} %param.13) | copy-start | bytes 9437188
  8.0 4.0 %copy-start.19 = (bf16[1,64,3072]{2,1,0:T(8,128)(2,1)S(1)}, bf16[1,64,3072]{2,1,0:T(8,128)(2,1)}, u32[]{:S(2)}) copy-start(bf16[1,64,3072]{2,1,0:T(8,128)(2,1)} %param.17) | copy-start | bytes 1179652
  8.0 34.0 %all-gather.2.cloned.1.call-start = ((), (), s32[]{:S(2)}) async-start(), calls=%async_computation.1 | async-start | bytes 2359296 | tf_op jit(solution)/shard_map/all_gather | solution.py:106
  11.9 99.4 %all-reduce.2.cloned.1.call-start = ((), (), s32[]{:S(2)}) async-start(), calls=%async_computation.3 | async-start | bytes 1572864 | tf_op jit(solution)/shard_map/psum | solution.py:185
  14.1 112.0 %reduce-scatter.2.cloned.1.call-start = ((), (), s32[]{:S(2)}) async-start(), calls=%async_computation.2 | async-start | bytes 2359296 | tf_op jit(solution)/shard_map/reduce_scatter | solution.py:165
  42.0 6.4 %copy-start.8 = (bf16[512,3072]{1,0:T(8,128)(2,1)S(1)}, bf16[512,3072]{1,0:T(8,128)(2,1)}, u32[]{:S(2)}) copy-start(bf16[512,3072]{1,0:T(8,128)(2,1)} %copy.35) | copy-start | bytes 9437188
  47.3 3.2 %copy-start.7 = (f32[256,8,128]{0,2,1:T(8,128)}, f32[256,8,128]{0,2,1:T(8,128)S(1)}, u32[]{:S(2)}) copy-start(f32[256,8,128]{0,2,1:T(8,128)S(1)} %fusion.26) | copy-start | bytes 3145732
  47.3 2.2 %copy-start.1 = (bf16[256,3072]{1,0:T(8,128)(2,1)S(1)}, bf16[256,3072]{1,0:T(8,128)(2,1)}, u32[]{:S(2)}) copy-start(bf16[256,3072]{1,0:T(8,128)(2,1)} %all-gather.2.cloned.1.call-done) | copy-start | bytes 4718596
  55.0 2.7 %copy-start.10 = (f32[256,4,128]{0,2,1:T(8,128)S(1)}, f32[256,4,128]{0,2,1:T(8,128)}, u32[]{:S(2)}) copy-start(f32[256,4,128]{0,2,1:T(8,128)} %copy-done.9) | copy-start | bytes 1572868
  55.0 2.7 %copy-start.14 = (f32[256,4,64]{0,2,1:T(8,128)S(1)}, f32[256,4,64]{0,2,1:T(8,128)}, u32[]{:S(2)}) copy-start(f32[256,4,64]{0,2,1:T(8,128)} %get-tuple-element.43) | copy-start | bytes 786436
  55.0 2.7 %copy-start.15 = (f32[256,4,64]{0,2,1:T(8,128)S(1)}, f32[256,4,64]{0,2,1:T(8,128)}, u32[]{:S(2)}) copy-start(f32[256,4,64]{0,2,1:T(8,128)} %get-tuple-element.44) | copy-start | bytes 786436
  55.0 3.5 %copy-start.11 = (bf16[1,256,1024]{1,2,0:T(8,128)(2,1)S(1)}, bf16[1,256,1024]{1,2,0:T(8,128)(2,1)}, u32[]{:S(2)}) copy-start(bf16[1,256,1024]{1,2,0:T(8,128)(2,1)} %copy.41) | copy-start | bytes 1572868
  55.0 3.5 %copy-start.16 = (bf16[256,4,128]{2,1,0:T(4,128)(2,1)S(1)}, bf16[256,4,128]{2,1,0:T(4,128)(2,1)}, u32[]{:S(2)}) copy-start(bf16[256,4,128]{2,1,0:T(4,128)(2,1)} %reshape.115) | copy-start | bytes 786436
  74.2 2.3 %copy-start.17 = (f32[256,4,128]{0,2,1:T(8,128)S(1)}, f32[256,4,128]{0,2,1:T(8,128)}, u32[]{:S(2)}) copy-start(f32[256,4,128]{0,2,1:T(8,128)} %get-tuple-element.49) | copy-start | bytes 1572868
  74.2 2.4 %copy-start.4 = (f32[4,128,2,256]{3,1,2,0:T(8,128)S(1)}, f32[4,128,2,256]{3,1,2,0:T(8,128)}, u32[]{:S(2)}) copy-start(f32[4,128,2,256]{3,1,2,0:T(8,128)} %fusion.44) | copy-start | bytes 3145732
  74.2 3.7 %slice-start = ((s8[6291456]{0:T(1024)(128)(4,1)}), s8[4194304]{0:T(1024)(128)(4,1)S(1)}, s32[]{:S(2)}) async-start(s8[6291456]{0:T(1024)(128)(4,1)} %bitcast.139), calls=%async_computation.4 | async-start | bytes 8388608
  76.5 5.6 %copy-start.12 = (bf16[4,256,128]{1,2,0:T(8,128)(2,1)}, bf16[4,256,128]{1,2,0:T(8,128)(2,1)S(1)}, u32[]{:S(2)}) copy-start(bf16[4,256,128]{1,2,0:T(8,128)(2,1)S(1)} %fusion.33) | copy-start | bytes 786436
  76.5 2.5 %slice-start.1 = ((s8[6291456]{0:T(1024)(128)(4,1)}), s8[2097152]{0:T(1024)(128)(4,1)S(1)}, s32[]{:S(2)}) async-start(s8[6291456]{0:T(1024)(128)(4,1)} %bitcast.139), calls=%async_computation.5 | async-start | bytes 4194304
  79.0 1.9 %copy-start.18 = (f32[256,4,128]{0,2,1:T(8,128)S(1)}, f32[256,4,128]{0,2,1:T(8,128)}, u32[]{:S(2)}) copy-start(f32[256,4,128]{0,2,1:T(8,128)} %get-tuple-element.50) | copy-start | bytes 1572868
  79.0 2.1 %copy-start.3 = (bf16[1,3072,512]{2,1,0:T(8,128)(2,1)S(1)}, bf16[1,3072,512]{2,1,0:T(8,128)(2,1)}, u32[]{:S(2)}) copy-start(bf16[1,3072,512]{2,1,0:T(8,128)(2,1)} %param.12) | copy-start | bytes 9437188
  111.3 3.1 %copy-start.5 = (f32[4,128,2,256]{3,1,2,0:T(8,128)S(1)}, f32[4,128,2,256]{3,1,2,0:T(8,128)}, u32[]{:S(2)}) copy-start(f32[4,128,2,256]{3,1,2,0:T(8,128)} %fusion.44) | copy-start | bytes 3145732
  111.3 3.1 %copy-start.6 = (f32[256,8,128]{0,2,1:T(8,128)S(1)}, f32[256,8,128]{0,2,1:T(8,128)}, u32[]{:S(2)}) copy-start(f32[256,8,128]{0,2,1:T(8,128)} %get-tuple-element.36) | copy-start | bytes 3145732
  114.5 1.4 copy-start.13
  121.5 4.6 %copy-start.20 = (f32[1,3072]{1,0:T(1,128)S(1)}, f32[1,3072]{1,0:T(1,128)}, u32[]{:S(2)}) copy-start(f32[1,3072]{1,0:T(1,128)} %param.10) | copy-start | bytes 36868
  (2 other events, 2.4 us)
Sparse Core Ops, SparseCore 0:
  12.1 29.9 all-gather.1
  84.5 26.1 reduce-scatter.1
Sparse Core Ops, SparseCore 1:
  16.4 94.9 all-reduce.1
where the time goes:
time: 148 us; the launch traced here: 147 us
  matrix products  41.3 us (28%)
  waiting for transfers between devices  38.9 us (26%)
  other arithmetic  21.3 us (14%)
  local copies, waits for them, and re-layouts  20.8 us (14%)
  between operations  15.7 us (11%)
  blocking collectives  8.76 us (6%)
    psum x1, waiting for transfers between devices, body(): mean_delta = lax.psum(delta, 'rep') / replicas  27 us
    all_gather x1, waiting for transfers between devices, body(): normalized = lax.all_gather(normalized_local, 'tp', axis=0, tiled=True)  11.8 us
    psum x1, blocking collectives, body(): lax.psum(jnp.sum(summed_rows * normalized_input, axis=0), 'tp')  8.76 us
    dot_general x1, local copies, waits for them, and re-layouts, body(): jnp.dot(normalized, weight_q, preferred_element_type=jnp.float32)  8.68 us
    dot_general x1, matrix products, one_block(): jnp.einsum('grqk,qgrd->kgd', score_low, query_block, preferred_element_ty...  5.36 us
    dot_general x1, matrix products, one_block(): jnp.einsum('grqk,kgd->qgrd', score_low, rotated_keys, preferred_element_t...  5.3 us
    dot_general x1, matrix products, body(): jnp.dot(normalized, weight_q, preferred_element_type=jnp.float32)  5.26 us
    dot_general x1, local copies, waits for them, and re-layouts, body(): jnp.dot(normalized, weight_k, preferred_element_type=jnp.float32)  4.69 us
  transfers between devices with their start and end apart: 3, of which 2 were waited for; matrix products, arithmetic and copies ran while one was open for 49% of the time, Pallas kernels for 0%

commit v1 on v0

--- a/solution.py
+++ b/solution.py
@@ -103,7 +103,13 @@
     )
     normalized_input = widened_rows * inverse_norm
     normalized_local = (normalized_input * norm_gains[None, :]).astype(jnp.bfloat16)
-    normalized = lax.all_gather(normalized_local, "tp", axis=0, tiled=True)
+    normalized = jnp.roll(
+        jnp.concatenate(
+            [normalized_local, lax.ppermute(normalized_local, "tp", [(0, 1), (1, 0)])], axis=0
+        ),
+        lax.axis_index("tp") * normalized_local.shape[0],
+        axis=0,
+    )
     sequence_length = normalized.shape[0]
     heads_q = weight_q.shape[1] // HEAD_SIZE
     heads_kv = weight_k.shape[1] // HEAD_SIZE

time: 148 us -> 145 us (0.980)
  waiting for transfers between devices: 38.9 us -> 32.6 us
  starting transfers between devices: 0.12 us -> 3.08 us
  other arithmetic: 21.3 us -> 23.4 us
    all_gather x1 -> x0, waiting for transfers between devices: 11.8 us -> none  [body(): normalized = lax.all_gather(normalized_local, 'tp', axis=0, tiled=True)]
    psum x1, waiting for transfers between devices: 27 us -> 31.6 us  [body(): mean_delta = lax.psum(delta, 'rep') / replicas]
    concatenate x0 -> x1, other arithmetic: none -> 3.09 us  [body(): jnp.roll(jnp.concatenate([normalized_local, lax.ppermute(normalized_local...]
    ppermute x0 -> x1, starting transfers between devices: none -> 3 us  [body(): lax.ppermute(normalized_local, 'tp', [(0, 1), (1, 0)])]
    unnamed x46 -> x48, local copies, waits for them, and re-layouts: 3.6 us -> 2.51 us
  transfers between devices with their start and end apart: 3 -> 3, of which waited for: 2 -> 2; matrix products, arithmetic and copies ran while one was open for 49% -> 51% of each run, Pallas kernels for 0% -> 0%
where the time goes in v1:
time: 145 us; the launch traced here: 144 us
  matrix products  41.3 us (28%)
  waiting for transfers between devices  32.6 us (22%)
  other arithmetic  23.4 us (16%)
  local copies, waits for them, and re-layouts  19.5 us (13%)
  between operations  15.7 us (11%)
  blocking collectives  8.59 us (6%)
  starting transfers between devices  3.08 us (2%)
    psum x1, waiting for transfers between devices, body(): mean_delta = lax.psum(delta, 'rep') / replicas  31.6 us
    dot_general x1, local copies, waits for them, and re-layouts, body(): jnp.dot(normalized, weight_q, preferred_element_type=jnp.float32)  8.62 us
    psum x1, blocking collectives, body(): lax.psum(jnp.sum(summed_rows * normalized_input, axis=0), 'tp')  8.59 us
    dot_general x1, matrix products, one_block(): jnp.einsum('grqk,qgrd->kgd', score_low, query_block, preferred_element_ty...  5.38 us
    dot_general x1, matrix products, one_block(): jnp.einsum('grqk,kgd->qgrd', score_low, rotated_keys, preferred_element_t...  5.29 us
    dot_general x1, matrix products, body(): jnp.dot(normalized, weight_q, preferred_element_type=jnp.float32)  5.28 us
    dot_general x1, local copies, waits for them, and re-layouts, body(): jnp.dot(normalized, weight_k, preferred_element_type=jnp.float32)  4.63 us
    dot_general x1, matrix products, body(): lax.dot_general(normalized, dquery, contract, preferred_element_type=jnp....  4.57 us
  transfers between devices with their start and end apart: 3, of which 2 were waited for; matrix products, arithmetic and copies ran while one was open for 51% of the time, Pallas kernels for 0%

profile of v1, /device:TPU:0, one launch (start us, length us, event | category | flops | bytes accessed | tf_op | source)
XLA Modules:
  0.0 144.3 jit_solution(2043605847415790632)
XLA Ops:
  9.6 2.3 %fusion.22 = bf16[128,3072]{1,0:T(8,128)(2,1)} fusion(bf16[1,128,3072]{2,1,0:T(8,128)(2,1)} %param.9, f32[3072]{0:T(1024)} %bitcast.153, f32[128]{0:T(128)S(1)} %add_rsqrt_fusion), kind=kLoop, calls=%fused_computation.38 | loop fusion | flops 1572864 | bytes 1585664 | tf_op jit(solution)/shard_map/convert_element_type | solution.py:105
  11.9 3.0 %collective-permute-start = (bf16[128,3072]{1,0:T(8,128)(2,1)}, bf16[128,3072]{1,0:T(8,128)(2,1)}, u32[]{:S(2)}, u32[]{:S(2)}) collective-permute-start(bf16[128,3072]{1,0:T(8,128)(2,1)} %fusion.22), channel_id=1, source_target_pairs={{0,1},{1,0},{2,3},{3,2},{4,5},{5,4},{6,7},{7,6},{8,9},{9,8},{10,11... | collective-permute-start | bytes 2359304 | tf_op jit(solution)/shard_map/ppermute | solution.py:108
  15.9 8.6 %copy.38 = bf16[1024,3072]{1,0:T(8,128)(2,1)} copy(bf16[1024,3072]{0,1:T(8,128)(2,1)} %bitcast.138) | data formatting | bytes 12582912 | tf_op jit(solution)/shard_map/dot_general | solution.py:117
  24.6 4.6 %copy.35 = bf16[512,3072]{1,0:T(8,128)(2,1)} copy(bf16[512,3072]{0,1:T(8,128)(2,1)} %bitcast.137) | data formatting | bytes 6291456 | tf_op jit(solution)/shard_map/dot_general | solution.py:121
  29.2 2.0 %copy.41 = bf16[1,256,1024]{1,2,0:T(8,128)(2,1)} copy(bf16[1,256,1024]{2,1,0:T(8,128)(2,1)} %param.14) | data formatting | bytes 1048576 | tf_op jit(solution)/shard_map/reshape;squeeze | solution.py:136
  32.7 3.1 %fusion.28 = bf16[256,3072]{1,0:T(8,128)(2,1)S(1)} fusion(s32[]{:T(128)S(6)} %select_n.22, bf16[128,3072]{1,0:T(8,128)(2,1)} %fusion.22, bf16[128,3072]{1,0:T(8,128)(2,1)} %collective-permute-done), kind=kLoop, calls=%fused_computation.44 | loop fusion | flops 6291456 | bytes 3145732 | tf_op jit(solution)/shard_map/jit(_roll_dynamic)/concatenate | solution.py:106
  35.9 5.3 %fusion.29 = f32[256,8,128]{0,2,1:T(8,128)S(1)} fusion(bf16[8,128,3072]{2,1,0:T(8,128)(2,1)} %bitcast.141, bf16[256,3072]{1,0:T(8,128)(2,1)S(1)} %fusion.28), kind=kOutput, calls=%fused_computation.45 | convolution fusion | flops 1610612736 | bytes 8912896 | tf_op jit(solution)/shard_map/dot_general | solution.py:117
  46.0 1.7 %reshape.115 = bf16[256,4,128]{2,1,0:T(4,128)(2,1)} reshape(bf16[256,512]{1,0:T(8,128)(2,1)} %fusion.33) | data formatting | bytes 524288 | tf_op jit(solution)/shard_map/reshape | solution.py:128
  47.8 2.7 %fusion.38 = bf16[256,8,128]{0,2,1:T(8,128)(2,1)} fusion(f32[256,8,64]{0,2,1:T(8,128)} %get-tuple-element.40, f32[256,8,64]{0,2,1:T(8,128)} %get-tuple-element.39, f32[256,8,128]{0,2,1:T(8,128)} %copy-done.7, f32[256,128]{0,1:T(8,128)S(1)} %get-tuple-element.46, f32[256,128]{0,1:T(8,128)S(1)} %get-tuple-element.45), kind=kLoop, calls=%fused_computation.55 | loop fusion | flops 1310720 | bytes 2883584 | tf_op jit(solution)/shard_map/convert_element_type | solution.py:120
  51.3 1.7 %fusion.54 = f32[4,256,256,2]{2,1,3,0:T(8,128)} fusion(bf16[256,4,2,128]{0,3,2,1:T(8,128)(2,1)S(1)} %bitcast.146, bf16[256,4,128,1]{2,1,0,3:T(4,128)(2,1)S(1)} %bitcast.149), kind=kOutput, calls=%fused_computation.85 | convolution fusion | flops 134217728 | bytes 2883584 | tf_op jit(solution)/shard_map/while/body/eval_jaxpr/qgrd,kgd->grqk/dot_general | solution.py:60
  53.1 3.3 %fusion.68 = (f32[4,2,256]{2,1,0:T(2,128)S(1)}, f32[4,2,256,256]{2,3,1,0:T(8,128)}) fusion(pred[256,256]{0,1:T(8,128)(4,1)S(1)} %iota_compare_fusion, bf16[256,4,128,1]{0,2,3,1:T(8,128)(2,1)} %fusion.53, bf16[256,4,2,128]{0,3,2,1:T(8,128)(2,1)} %bitcast.150), kind=kOutput, calls=%fused_computation.105 | convolution fusion | flops 136315136 | bytes 2957312 | tf_op jit(solution)/shard_map/while/body/eval_jaxpr/sub | solution.py:54
  56.3 5.4 %broadcast_multiply_fusion = (f32[256,4,128]{0,2,1:T(8,128)}, f32[256,4,128]{0,2,1:T(8,128)}) fusion(f32[256,128]{0,1:T(8,128)S(1)} %get-tuple-element.46, bf16[256,4,2,128]{0,3,2,1:T(8,128)(2,1)} %bitcast.151, f32[4,256,256,2]{2,1,3,0:T(8,128)} %fusion.54, f32[4,2,256,256]{2,3,1,0:T(8,128)} %get-tuple-element.48, f32[4,2,256]{2,1,0:T(2,128)S(1)} %get-tuple-element.47), kind=kOutput, calls=%fused_computation.88 | convolution fusion | flops 138021120 | bytes 5906432 | tf_op jit(solution)/shard_map/while/body/eval_jaxpr/grqk,qgrd->kgd/dot_general | solution.py:72
  61.7 5.3 %fusion.47 = f32[4,128,2,256]{3,1,2,0:T(8,128)} fusion(bf16[256,4,128,1]{0,2,3,1:T(8,128)(2,1)} %fusion.53, f32[4,256,256,2]{2,1,3,0:T(8,128)} %fusion.54, f32[4,2,256,256]{2,3,1,0:T(8,128)} %get-tuple-element.48, f32[4,2,256]{2,1,0:T(2,128)S(1)} %get-tuple-element.47), kind=kOutput, calls=%fused_computation.69 | convolution fusion | flops 137890048 | bytes 5513216 | tf_op jit(solution)/shard_map/while/body/eval_jaxpr/grqk,kgd->qgrd/dot_general | solution.py:69
  67.0 2.3 %fusion.36 = bf16[4,256,128]{1,2,0:T(8,128)(2,1)S(1)} fusion(bf16[256,4,2,128]{0,3,2,1:T(8,128)(2,1)} %bitcast.145, f32[4,2,256,256]{2,3,1,0:T(8,128)} %get-tuple-element.48, f32[4,2,256]{2,1,0:T(2,128)S(1)} %get-tuple-element.47), kind=kOutput, calls=%fused_computation.52 | convolution fusion | flops 135397376 | bytes 2891776 | tf_op jit(solution)/shard_map/while/body/eval_jaxpr/grqk,qgrd->kgd/dot_general | solution.py:57
  71.8 1.8 %fusion.2 = f32[256,3072]{1,0:T(8,128)S(1)} fusion(bf16[256,1024]{0,1:T(8,128)(2,1)S(1)} %bitcast.152, bf16[1,3072,1024]{2,1,0:T(8,128)(2,1)S(1)} %bitcast.140), kind=kOutput, calls=%fused_computation.2 | convolution fusion | flops 1610612736 | bytes 9961472 | tf_op jit(solution)/shard_map/dot_general | solution.py:167
  75.2 2.2 %fusion.6 = bf16[256,3072]{1,0:T(8,128)(2,1)} fusion(f32[256,3072]{1,0:T(8,128)S(1)} %convolution_add_fusion.1, bf16[256,512]{0,1:T(8,128)(2,1)S(1)} %bitcast.147, bf16[1,3072,512]{2,1,0:T(8,128)(2,1)S(1)} %copy-done), kind=kOutput, calls=%fused_computation.11 | convolution fusion | flops 806879232 | bytes 8126464 | tf_op jit(solution)/shard_map/dot_general | solution.py:174
  77.4 31.6 %all-reduce.2.cloned.1.call-done = f32[64,3072]{1,0:T(8,128)} async-done(((f32[64,3072]{1,0:T(8,128)}), f32[64,3072]{1,0:T(8,128)}) %all-reduce.2.cloned.1.call-update) | async-done | bytes 786448 | tf_op jit(solution)/shard_map/psum | solution.py:191
  109.1 3.1 %multiply_subtract_fusion = (f32[64,3072]{1,0:T(8,128)}, f32[64,3072]{1,0:T(8,128)}) fusion(f32[64,3072]{1,0:T(8,128)} %param.15, f32[64,3072]{1,0:T(8,128)} %all-reduce.2.cloned.1.call-done, f32[64,3072]{1,0:T(8,128)} %param.16), kind=kLoop, calls=%fused_computation.73 | loop fusion | flops 1376256 | bytes 3932160 | tf_op jit(solution)/shard_map/sub | solution.py:193
  113.6 2.7 %fusion.5 = bf16[1,3072,512]{2,1,0:T(8,128)(2,1)} fusion(bf16[256,3072]{1,0:T(8,128)(2,1)S(1)} %copy-done.2, bf16[256,512]{0,1:T(8,128)(2,1)S(1)} %bitcast.148), kind=kOutput, calls=%fused_computation.8 | convolution fusion | flops 806879232 | bytes 4980736 | tf_op jit(solution)/shard_map/dot_general | solution.py:163
  116.3 2.7 %fusion.4 = bf16[1,3072,512]{2,1,0:T(8,128)(2,1)} fusion(bf16[256,3072]{1,0:T(8,128)(2,1)S(1)} %copy-done.2, bf16[256,512]{0,1:T(8,128)(2,1)S(1)} %bitcast.144), kind=kOutput, calls=%fused_computation.7 | convolution fusion | flops 806879232 | bytes 4980736 | tf_op jit(solution)/shard_map/dot_general | solution.py:160
  119.0 4.6 %convert_bitcast_fusion = bf16[1,3072,1024]{2,1,0:T(8,128)(2,1)} fusion(bf16[256,3072]{1,0:T(8,128)(2,1)S(1)} %copy-done.2, bf16[256,1024]{0,1:T(8,128)(2,1)S(1)} %fusion.40), kind=kOutput, calls=%fused_computation.4 | convolution fusion | flops 1613758464 | bytes 8388608 | tf_op jit(solution)/shard_map/dot_general | solution.py:157
  123.6 1.9 %fusion.24 = (f32[128]{0:T(128)S(1)}, f32[3072]{0:T(1024)S(1)}) fusion(bf16[128,3072]{1,0:T(8,128)(2,1)} %reduce-scatter.2.cloned.1.call-done, bf16[1,128,3072]{2,1,0:T(8,128)(2,1)} %param.9, f32[3072]{0:T(1024)S(1)} %bitcast.154, f32[128]{0:T(128)S(1)} %add_rsqrt_fusion), kind=kLoop, calls=%fused_computation.40 | loop fusion | flops 3142528 | bytes 1598464 | tf_op jit(solution)/shard_map/reduce_sum | solution.py:186
  125.5 8.6 %psum.14 = f32[1,3072]{1,0:T(1,128)} all-reduce(f32[1,3072]{1,0:T(1,128)S(1)} %bitcast.156), channel_id=1, replica_groups=mesh['rep'=16,'tp'=2] {'tp'}, use_global_device_ids=true, to_apply=%region_6.7 | all-reduce | flops 3072 | bytes 24576 | tf_op jit(solution)/shard_map/psum | solution.py:180
  134.1 2.7 %fusion.49 = bf16[1,128,3072]{2,1,0:T(8,128)(2,1)} fusion(bf16[128,3072]{1,0:T(8,128)(2,1)} %reduce-scatter.2.cloned.1.call-done, bf16[1,128,3072]{2,1,0:T(8,128)(2,1)} %param.9, f32[128]{0:T(128)S(1)} %broadcast_multiply_fusion.1, f32[3072]{0:T(1024)S(1)} %bitcast.155, f32[128]{0:T(128)S(1)} %add_rsqrt_fusion), kind=kLoop, calls=%fused_computation.71 | loop fusion | flops 3145728 | bytes 2372608 | tf_op jit(solution)/shard_map/broadcast_in_dim | solution.py:199
  (75 shorter events, 15.1 us)
Async XLA Ops:
  8.0 36.3 %copy-start = (bf16[1,3072,512]{2,1,0:T(8,128)(2,1)S(1)}, bf16[1,3072,512]{2,1,0:T(8,128)(2,1)}, u32[]{:S(2)}) copy-start(bf16[1,3072,512]{2,1,0:T(8,128)(2,1)} %param.13) | copy-start | bytes 9437188
  8.0 6.9 %copy-start.20 = (bf16[1,64,3072]{2,1,0:T(8,128)(2,1)S(1)}, bf16[1,64,3072]{2,1,0:T(8,128)(2,1)}, u32[]{:S(2)}) copy-start(bf16[1,64,3072]{2,1,0:T(8,128)(2,1)} %param.17) | copy-start | bytes 1179652
  8.0 101.0 %all-reduce.2.cloned.1.call-start = ((), (), s32[]{:S(2)}) async-start(), calls=%async_computation.2 | async-start | bytes 1572864 | tf_op jit(solution)/shard_map/psum | solution.py:191
  8.1 6.8 %copy-start.9 = (f32[64,3072]{1,0:T(8,128)S(1)}, f32[64,3072]{1,0:T(8,128)}, u32[]{:S(2)}) copy-start(f32[64,3072]{1,0:T(8,128)} %param.15) | copy-start | bytes 2359300
  11.9 20.8 %collective-permute-start = (bf16[128,3072]{1,0:T(8,128)(2,1)}, bf16[128,3072]{1,0:T(8,128)(2,1)}, u32[]{:S(2)}, u32[]{:S(2)}) collective-permute-start(bf16[128,3072]{1,0:T(8,128)(2,1)} %fusion.22), channel_id=1, source_target_pairs={{0,1},{1,0},{2,3},{3,2},{4,5},{5,4},{6,7},{7,6},{8,9},{9,8},{10,11... | collective-permute-start | bytes 2359304 | tf_op jit(solution)/shard_map/ppermute | solution.py:108
  15.9 107.7 %reduce-scatter.2.cloned.1.call-start = ((), (), s32[]{:S(2)}) async-start(), calls=%async_computation.1 | async-start | bytes 2359296 | tf_op jit(solution)/shard_map/reduce_scatter | solution.py:171
  35.8 8.5 %copy-start.1 = (bf16[256,3072]{1,0:T(8,128)(2,1)}, bf16[256,3072]{1,0:T(8,128)(2,1)S(1)}, u32[]{:S(2)}) copy-start(bf16[256,3072]{1,0:T(8,128)(2,1)S(1)} %fusion.28) | copy-start | bytes 4718596
  35.9 6.4 %copy-start.8 = (bf16[512,3072]{1,0:T(8,128)(2,1)S(1)}, bf16[512,3072]{1,0:T(8,128)(2,1)}, u32[]{:S(2)}) copy-start(bf16[512,3072]{1,0:T(8,128)(2,1)} %copy.35) | copy-start | bytes 9437188
  41.1 2.2 %copy-start.7 = (f32[256,8,128]{0,2,1:T(8,128)}, f32[256,8,128]{0,2,1:T(8,128)S(1)}, u32[]{:S(2)}) copy-start(f32[256,8,128]{0,2,1:T(8,128)S(1)} %fusion.29) | copy-start | bytes 3145732
  47.8 2.7 %copy-start.11 = (f32[256,4,128]{0,2,1:T(8,128)S(1)}, f32[256,4,128]{0,2,1:T(8,128)}, u32[]{:S(2)}) copy-start(f32[256,4,128]{0,2,1:T(8,128)} %copy-done.10) | copy-start | bytes 1572868
  47.8 2.7 %copy-start.15 = (f32[256,4,64]{0,2,1:T(8,128)S(1)}, f32[256,4,64]{0,2,1:T(8,128)}, u32[]{:S(2)}) copy-start(f32[256,4,64]{0,2,1:T(8,128)} %get-tuple-element.43) | copy-start | bytes 786436
  47.8 2.7 %copy-start.16 = (f32[256,4,64]{0,2,1:T(8,128)S(1)}, f32[256,4,64]{0,2,1:T(8,128)}, u32[]{:S(2)}) copy-start(f32[256,4,64]{0,2,1:T(8,128)} %get-tuple-element.44) | copy-start | bytes 786436
  47.8 3.5 %copy-start.12 = (bf16[1,256,1024]{1,2,0:T(8,128)(2,1)S(1)}, bf16[1,256,1024]{1,2,0:T(8,128)(2,1)}, u32[]{:S(2)}) copy-start(bf16[1,256,1024]{1,2,0:T(8,128)(2,1)} %copy.41) | copy-start | bytes 1572868
  47.8 3.5 %copy-start.17 = (bf16[256,4,128]{2,1,0:T(4,128)(2,1)S(1)}, bf16[256,4,128]{2,1,0:T(4,128)(2,1)}, u32[]{:S(2)}) copy-start(bf16[256,4,128]{2,1,0:T(4,128)(2,1)} %reshape.115) | copy-start | bytes 786436
  67.0 2.4 %copy-start.18 = (f32[256,4,128]{0,2,1:T(8,128)S(1)}, f32[256,4,128]{0,2,1:T(8,128)}, u32[]{:S(2)}) copy-start(f32[256,4,128]{0,2,1:T(8,128)} %get-tuple-element.49) | copy-start | bytes 1572868
  67.0 2.4 %copy-start.4 = (f32[4,128,2,256]{3,1,2,0:T(8,128)S(1)}, f32[4,128,2,256]{3,1,2,0:T(8,128)}, u32[]{:S(2)}) copy-start(f32[4,128,2,256]{3,1,2,0:T(8,128)} %fusion.47) | copy-start | bytes 3145732
  67.0 3.7 %slice-start = ((s8[6291456]{0:T(1024)(128)(4,1)}), s8[4194304]{0:T(1024)(128)(4,1)S(1)}, s32[]{:S(2)}) async-start(s8[6291456]{0:T(1024)(128)(4,1)} %bitcast.139), calls=%async_computation.3 | async-start | bytes 8388608
  69.3 5.8 %copy-start.13 = (bf16[4,256,128]{1,2,0:T(8,128)(2,1)}, bf16[4,256,128]{1,2,0:T(8,128)(2,1)S(1)}, u32[]{:S(2)}) copy-start(bf16[4,256,128]{1,2,0:T(8,128)(2,1)S(1)} %fusion.36) | copy-start | bytes 786436
  69.4 2.5 %slice-start.1 = ((s8[6291456]{0:T(1024)(128)(4,1)}), s8[2097152]{0:T(1024)(128)(4,1)S(1)}, s32[]{:S(2)}) async-start(s8[6291456]{0:T(1024)(128)(4,1)} %bitcast.139), calls=%async_computation.4 | async-start | bytes 4194304
  71.8 1.9 %copy-start.19 = (f32[256,4,128]{0,2,1:T(8,128)S(1)}, f32[256,4,128]{0,2,1:T(8,128)}, u32[]{:S(2)}) copy-start(f32[256,4,128]{0,2,1:T(8,128)} %get-tuple-element.50) | copy-start | bytes 1572868
  71.8 2.1 %copy-start.3 = (bf16[1,3072,512]{2,1,0:T(8,128)(2,1)S(1)}, bf16[1,3072,512]{2,1,0:T(8,128)(2,1)}, u32[]{:S(2)}) copy-start(bf16[1,3072,512]{2,1,0:T(8,128)(2,1)} %param.12) | copy-start | bytes 9437188
  109.1 3.1 %copy-start.5 = (f32[4,128,2,256]{3,1,2,0:T(8,128)S(1)}, f32[4,128,2,256]{3,1,2,0:T(8,128)}, u32[]{:S(2)}) copy-start(f32[4,128,2,256]{3,1,2,0:T(8,128)} %fusion.47) | copy-start | bytes 3145732
  109.1 3.1 %copy-start.6 = (f32[256,8,128]{0,2,1:T(8,128)S(1)}, f32[256,8,128]{0,2,1:T(8,128)}, u32[]{:S(2)}) copy-start(f32[256,8,128]{0,2,1:T(8,128)} %get-tuple-element.36) | copy-start | bytes 3145732
  119.0 4.6 %copy-start.21 = (f32[1,3072]{1,0:T(1,128)S(1)}, f32[1,3072]{1,0:T(1,128)}, u32[]{:S(2)}) copy-start(f32[1,3072]{1,0:T(1,128)} %param.10) | copy-start | bytes 36868
  (3 other events, 3.8 us)
Sparse Core Ops, SparseCore 0:
  16.0 93.0 all-reduce.1
Sparse Core Ops, SparseCore 1:
  77.5 27.5 reduce-scatter.1
